TPU v7x, 32 devices: a whole 2x2x4 slice. The times are simulated.
32 devices in a mesh: section: 2 (over x), tensor: 2 (over y), expert: 8 (over z, core).
Axes of the slice: x: 2, y: 2, z: 4, core: 2. Of those that a mesh axis runs over, the one named last changes fastest.
Arguments:
- saved_inputs: bfloat16 [2, 2, 512, 2048], P('section', None, 'expert', 'tensor'), may hold values from -64 to 64
- cot_in: bfloat16 [2, 512, 2048], P('section', 'expert', 'tensor'), may hold values from -6 to 6
- loss_grad: bfloat16 [512, 2048], P('expert', 'tensor'), may hold values from -6 to 6
- expert_ids: int32 [2, 2, 512, 2], P('section', None, 'expert'), may hold values from 0 to 3, all different within a row; in each aligned block of 64 rows (0 to 63, 64 to 127, ..., all dimensions but the last counted through in order) at most 48 rows name the same one
- route_weights: float32 [2, 2, 512, 2], P('section', None, 'expert'), may hold values from 0.05 to 0.5
- norm_gain: float32 [2, 2048], P('section', 'tensor'), may hold values from 0.12 to 8
- w_gate: bfloat16 [2, 8, 2048, 384], P('section', 'expert', 'tensor'), may hold values from -0.125 to 0.125
- w_up: bfloat16 [2, 8, 2048, 384], P('section', 'expert', 'tensor'), may hold values from -0.125 to 0.125
- w_down: bfloat16 [2, 8, 384, 2048], P('section', 'expert', None, 'tensor'), may hold values from -0.21875 to 0.21875
Outputs:
- input_grads: bfloat16 [2, 2, 512, 2048], P('section', None, 'expert', 'tensor')
Inputs may be any that keep to these rules, and one draw needn't show every extreme that they name: `expert_ids`: each row names 2 different experts. Within each aligned block of 64 rows (the rows of one device in one micro-batch of one layer) no expert is named by more than 48 rows, and in some blocks one expert is named by exactly 48.
All inputs are finite; a program needn't handle non-finite values.
Results may differ from a plain program's by a relative error of at most 0.028.
Values may be sent and summed in bfloat16 or wider, within the bound.
A program may use at most 64 MiB of HBM per device.

v0:
```python
import jax
import jax.numpy as jnp
from jax import lax
from jax.sharding import PartitionSpec as P

D = 2048


epsilon = 1e-06


def from_partner(block, axis, stride):
    count = lax.axis_size(axis)
    route = []
    for low in range(count):
        high = low | 1 << stride
        if high != low and high < count:
            route += [(low, high), (high, low)]
    return lax.ppermute(block, axis, route)


def passed_along(array, axis, by):
    peers = lax.axis_size(axis)
    pairs = [(i, i + by) for i in range(peers) if 0 <= i + by < peers]
    return lax.ppermute(array, axis, pairs)


def silu_grad(values):
    sigma = jax.nn.sigmoid(values)
    return sigma * (1.0 + values * (1.0 - sigma))


def contract_last(left, right):
    return lax.dot_general(
        left, right, (((1,), (1,)), ((), ())), preferred_element_type=jnp.float32
    )


def send_back(grad_rows):
    return lax.all_to_all(grad_rows, "expert", split_axis=0, concat_axis=0, tiled=True)


def expert_rows(rows_in, rows_grad, gate_weights, up_weights, down_weights):
    sources, row_count, feat_width = rows_in.shape
    flat_in = rows_in.reshape(sources * row_count, feat_width)
    flat_grad = rows_grad.reshape(sources * row_count, feat_width)
    gate_part = jnp.dot(flat_in, gate_weights, preferred_element_type=jnp.float32)
    up_part = jnp.dot(flat_in, up_weights, preferred_element_type=jnp.float32)
    hidden_part = contract_last(flat_grad, down_weights)
    gate_sum, up_sum, hidden = (
        lax.psum(gate_part.astype(jnp.bfloat16), "tensor").astype(jnp.float32),
        lax.psum(up_part.astype(jnp.bfloat16), "tensor").astype(jnp.float32),
        lax.psum(hidden_part.astype(jnp.bfloat16), "tensor").astype(jnp.float32),
    )
    grad_gate = (hidden * up_sum * silu_grad(gate_sum)).astype(jnp.bfloat16)
    grad_up = (hidden * jax.nn.silu(gate_sum)).astype(jnp.bfloat16)
    grad_piece = contract_last(grad_gate, gate_weights) + contract_last(grad_up, up_weights)
    return grad_piece.astype(jnp.bfloat16).reshape(sources, row_count, feat_width)


def local(
    saved_inputs, cot_in, loss_grad, expert_ids, route_weights, norm_gain, w_gate, w_up, w_down
):
    section_count = lax.axis_size("section")
    at_last = lax.axis_index("section") == section_count - 1
    experts = lax.axis_size("expert") // 2
    tok_rows = saved_inputs.shape[2]
    feat_width = saved_inputs.shape[3]
    per_token = expert_ids.shape[3]
    capacity = 3 * tok_rows * per_token // (2 * experts)
    half_slots = capacity // 2
    gain_row = norm_gain[0][None, :]
    gate_weights = w_gate[0, 0]
    up_weights = w_up[0, 0]
    down_weights = w_down[0, 0]
    inputs = saved_inputs[0].astype(jnp.float32)
    squares = lax.psum(jnp.sum(inputs * inputs, axis=2), "tensor")
    root_mean = jnp.sqrt(squares / D + epsilon)[:, :, None]
    normed = inputs / root_mean

    def layer_step(micro, incoming):
        expert_input = (normed[micro] * gain_row).astype(jnp.bfloat16)
        flat_ids = expert_ids[0, micro].reshape(-1)
        onehot = (flat_ids[:, None] == jnp.arange(experts, dtype=jnp.int32)[None, :]).astype(
            jnp.int32
        )
        before = jnp.cumsum(onehot, axis=0) - onehot
        position = jnp.sum(before * onehot, axis=1)
        slot_index = flat_ids * capacity + position
        token_index = jnp.repeat(jnp.arange(tok_rows, dtype=jnp.int32), per_token)
        token_of = (
            jnp.full((experts * capacity,), tok_rows, jnp.int32).at[slot_index].set(token_index)
        )
        weight_of = (
            jnp.zeros((experts * capacity,), jnp.float32)
            .at[slot_index]
            .set(route_weights[0, micro].reshape(-1))
        )
        padded_input = jnp.concatenate(
            [expert_input, jnp.zeros((1, feat_width), jnp.bfloat16)], axis=0
        )
        padded_grad = jnp.concatenate([incoming, jnp.zeros((1, feat_width), jnp.bfloat16)], axis=0)
        send_normed = padded_input[token_of]
        send_grads = (weight_of[:, None] * padded_grad[token_of].astype(jnp.float32)).astype(
            jnp.bfloat16
        )
        send_normed = send_normed.reshape(2 * experts, half_slots, feat_width)
        send_grads = send_grads.reshape(2 * experts, half_slots, feat_width)
        pieces = (
            lax.all_to_all(send_normed, "expert", split_axis=0, concat_axis=0, tiled=True),
            lax.all_to_all(send_grads, "expert", split_axis=0, concat_axis=0, tiled=True),
        )
        partner_normed, partner_grads = from_partner((pieces[0], pieces[1]), "expert", 0)
        joined_normed = jnp.concatenate([pieces[0], partner_normed], axis=1)
        joined_grads = jnp.concatenate([pieces[1], partner_grads], axis=1)
        grad_rows = expert_rows(joined_normed, joined_grads, gate_weights, up_weights, down_weights)
        sources, row_count, width_here = pieces[0].shape
        gathered = send_back(grad_rows.reshape(sources, 2, row_count, width_here))
        flat_rows = gathered.reshape(-1, feat_width)
        which_half = position // half_slots
        within = position % half_slots
        first_index = (4 * flat_ids + which_half) * half_slots + within
        second_index = (4 * flat_ids + 3 - which_half) * half_slots + within
        first_rows = jnp.take(flat_rows, first_index, axis=0).astype(jnp.float32)
        second_rows = jnp.take(flat_rows, second_index, axis=0).astype(jnp.float32)
        cot_normed = jnp.sum(
            (first_rows + second_rows).reshape(tok_rows, per_token, feat_width), axis=1
        )
        scaled = gain_row * cot_normed
        inner = lax.psum(jnp.sum(normed[micro] * scaled, axis=1), "tensor")
        result = (
            incoming.astype(jnp.float32)
            + (scaled - normed[micro] * (inner / D)[:, None]) / root_mean[micro]
        )
        return result.astype(jnp.bfloat16)

    first_grads = layer_step(0, cot_in[0])
    passed = passed_along(first_grads, "section", -1)
    second_grads = layer_step(1, jnp.where(at_last, loss_grad, passed))
    return jnp.stack([first_grads, second_grads])[None]


def solution(mesh):
    in_specs = (
        P("section", None, "expert", "tensor"),
        P("section", "expert", "tensor"),
        P("expert", "tensor"),
        P("section", None, "expert", None),
        P("section", None, "expert", None),
        P("section", "tensor"),
        P("section", "expert", "tensor", None),
        P("section", "expert", "tensor", None),
        P("section", "expert", None, "tensor"),
    )
    out_specs = P("section", None, "expert", "tensor")
    return jax.shard_map(local, mesh=mesh, in_specs=in_specs, out_specs=out_specs, check_vma=False)
```

profile of v0, /device:TPU:0, one launch (start us, length us, event | category | flops | bytes accessed | tf_op | source)
XLA Modules:
  0.0 247.8 jit_solution(4345937539465168269)
XLA Ops:
  6.5 0.8 fusion.67
  7.6 0.2 reduce_window_sum.17
  7.8 0.2 select_reduce_fusion.1
  8.1 0.1 mul.183
  8.4 1.0 scatter_custom_fusion.1
  9.4 1.1 fusion.30
  10.5 5.9 %psum.64 = f32[2,64]{1,0:T(2,128)S(1)} all-reduce(f32[2,64]{1,0:T(2,128)S(1)} %fusion.30), channel_id=1, replica_groups=mesh['section'=2,'tensor'=2,'expert'=8] {'tensor'}, use_global_device_ids=true, to_apply=%region_6.7 | all-reduce | flops 128 | bytes 1024 | tf_op jit(solution)/shard_map/psum | solution.py:77
  16.4 1.1 convert_divide_fusion
  17.5 0.7 fusion.42
  18.2 1.8 gather_fusion.1
  20.0 5.4 %all-to-all-start.1 = ((bf16[8,24,1024]{2,1,0:T(8,128)(2,1)}), bf16[8,24,1024]{2,1,0:T(8,128)(2,1)S(1)}, u32[]{:S(2)}, u32[]{:S(2)}) async-start(bf16[8,24,1024]{2,1,0:T(8,128)(2,1)} %bitcast.10), calls=%async_computation.1 | async-start | bytes 786432 | tf_op jit(solution)/shard_map/all_to_all | solution.py:110
  25.4 1.0 gather_fusion
  26.7 1.0 scatter_custom_fusion
  27.7 0.9 fusion.1
  28.6 9.3 %all-to-all-done.1 = bf16[8,24,1024]{2,1,0:T(8,128)(2,1)S(1)} async-done(((bf16[8,24,1024]{2,1,0:T(8,128)(2,1)}), bf16[8,24,1024]{2,1,0:T(8,128)(2,1)S(1)}, u32[]{:S(2)}, u32[]{:S(2)}) %all-to-all-start.1) | async-done | bytes 393248 | tf_op jit(solution)/shard_map/all_to_all | solution.py:110
  37.9 3.5 %all-to-all-start = ((bf16[8,24,1024]{2,1,0:T(8,128)(2,1)}), bf16[8,24,1024]{2,1,0:T(8,128)(2,1)S(1)}, u32[]{:S(2)}, u32[]{:S(2)}) async-start(bf16[8,24,1024]{2,1,0:T(8,128)(2,1)} %fusion.1), calls=%async_computation | async-start | bytes 786432 | tf_op jit(solution)/shard_map/all_to_all | solution.py:111
  41.4 0.4 collective-permute-start.1
  41.8 12.0 %all-to-all-done = bf16[8,24,1024]{2,1,0:T(8,128)(2,1)S(1)} async-done(((bf16[8,24,1024]{2,1,0:T(8,128)(2,1)}), bf16[8,24,1024]{2,1,0:T(8,128)(2,1)S(1)}, u32[]{:S(2)}, u32[]{:S(2)}) %all-to-all-start) | async-done | bytes 393248 | tf_op jit(solution)/shard_map/all_to_all | solution.py:111
  53.9 1.3 convolution_convert_fusion.3
  55.2 1.3 convolution_convert_fusion.4
  56.5 1.3 convolution_convert_fusion.5
  58.2 0.2 reduce_window_sum.18
  58.6 0.2 select_reduce_fusion
  58.8 34.9 %all-reduce.11.cloned.1.call-done = (bf16[384,384]{1,0:T(8,128)(2,1)}, bf16[384,384]{1,0:T(8,128)(2,1)}, bf16[384,384]{1,0:T(8,128)(2,1)}) async-done(((bf16[384,384]{1,0:T(8,128)(2,1)}, bf16[384,384]{1,0:T(8,128)(2,1)}, bf16[384,384]{1,0:T(8,128)(2,1)}), (bf16[384,384]{1,0:T(8,128)(2,1)}, bf16[384,384]{1,0:T(8,128)(2,1)}, bf16[384,384]{1,0:T(8,128)(2,1)})) %all-reduce.11.cloned.1.call-update) | async-done | bytes 884752 | tf_op jit(solution)/shard_map/psum | solution.py:53
  93.7 1.9 fusion.5
  95.6 1.5 add_convert_fusion.1
  97.1 4.6 %all-to-all-start.2 = ((bf16[8,2,24,1024]{3,2,1,0:T(8,128)(2,1)}), bf16[8,2,24,1024]{3,2,1,0:T(8,128)(2,1)S(1)}, u32[]{:S(2)}, u32[]{:S(2)}) async-start(bf16[8,2,24,1024]{3,2,1,0:T(8,128)(2,1)} %bitcast.14), calls=%async_computation.2 | async-start | bytes 1572864 | tf_op jit(solution)/shard_map/all_to_all | solution.py:40
  101.7 1.0 scatter_custom_fusion.3
  102.8 19.8 %all-to-all-done.2 = bf16[8,2,24,1024]{3,2,1,0:T(8,128)(2,1)S(1)} async-done(((bf16[8,2,24,1024]{3,2,1,0:T(8,128)(2,1)}), bf16[8,2,24,1024]{3,2,1,0:T(8,128)(2,1)S(1)}, u32[]{:S(2)}, u32[]{:S(2)}) %all-to-all-start.2) | async-done | bytes 786464 | tf_op jit(solution)/shard_map/all_to_all | solution.py:40
  122.6 0.9 gather_fusion.4
  123.5 0.9 gather_fusion.5
  124.4 0.2 convert_add_fusion.1
  124.5 0.3 reshape.177
  124.8 0.6 reduce_sum.72
  125.5 0.1 fusion.43
  125.6 4.9 %psum.67 = f32[64]{0:T(128)S(1)} all-reduce(f32[64]{0:T(128)S(1)} %fusion.43), channel_id=1, replica_groups=mesh['section'=2,'tensor'=2,'expert'=8] {'tensor'}, use_global_device_ids=true, to_apply=%region_11.13 | all-reduce | flops 64 | bytes 512 | tf_op jit(solution)/shard_map/psum | solution.py:130
  130.7 1.8 gather_fusion.3
  132.5 3.5 %all-to-all-start.4 = ((bf16[8,24,1024]{2,1,0:T(8,128)(2,1)}), bf16[8,24,1024]{2,1,0:T(8,128)(2,1)S(1)}, u32[]{:S(2)}, u32[]{:S(2)}) async-start(bf16[8,24,1024]{2,1,0:T(8,128)(2,1)} %bitcast.23), calls=%async_computation.4 | async-start | bytes 786432 | tf_op jit(solution)/shard_map/all_to_all | solution.py:110
  135.9 1.3 collective-permute-start.2
  137.5 1.0 scatter_custom_fusion.2
  138.5 5.1 %collective-permute-done.2 = bf16[64,1024]{1,0:T(8,128)(2,1)S(1)} collective-permute-done((bf16[64,1024]{1,0:T(8,128)(2,1)S(1)}, bf16[64,1024]{1,0:T(8,128)(2,1)S(1)}, u32[]{:S(2)}, u32[]{:S(2)}) %collective-permute-start.2) | collective-permute-done | bytes 131104 | tf_op jit(solution)/shard_map/ppermute | solution.py:25
  143.7 1.0 gather_fusion.2
  144.7 0.9 fusion
  145.6 2.8 %all-to-all-done.4 = bf16[8,24,1024]{2,1,0:T(8,128)(2,1)S(1)} async-done(((bf16[8,24,1024]{2,1,0:T(8,128)(2,1)}), bf16[8,24,1024]{2,1,0:T(8,128)(2,1)S(1)}, u32[]{:S(2)}, u32[]{:S(2)}) %all-to-all-start.4) | async-done | bytes 393248 | tf_op jit(solution)/shard_map/all_to_all | solution.py:110
  148.4 3.5 %all-to-all-start.3 = ((bf16[8,24,1024]{2,1,0:T(8,128)(2,1)}), bf16[8,24,1024]{2,1,0:T(8,128)(2,1)S(1)}, u32[]{:S(2)}, u32[]{:S(2)}) async-start(bf16[8,24,1024]{2,1,0:T(8,128)(2,1)} %fusion), calls=%async_computation.3 | async-start | bytes 786432 | tf_op jit(solution)/shard_map/all_to_all | solution.py:111
  151.8 0.2 all-reduce.9.cloned.1.call-start
  152.1 0.2 collective-permute-start.4
  152.3 12.0 %all-to-all-done.3 = bf16[8,24,1024]{2,1,0:T(8,128)(2,1)S(1)} async-done(((bf16[8,24,1024]{2,1,0:T(8,128)(2,1)}), bf16[8,24,1024]{2,1,0:T(8,128)(2,1)S(1)}, u32[]{:S(2)}, u32[]{:S(2)}) %all-to-all-start.3) | async-done | bytes 393248 | tf_op jit(solution)/shard_map/all_to_all | solution.py:111
  164.4 1.3 convolution_convert_fusion
  165.7 1.3 convolution_convert_fusion.1
  167.0 1.3 convolution_convert_fusion.2
  168.4 34.8 %all-reduce.9.cloned.1.call-done = (bf16[384,384]{1,0:T(8,128)(2,1)}, bf16[384,384]{1,0:T(8,128)(2,1)}, bf16[384,384]{1,0:T(8,128)(2,1)}) async-done(((bf16[384,384]{1,0:T(8,128)(2,1)}, bf16[384,384]{1,0:T(8,128)(2,1)}, bf16[384,384]{1,0:T(8,128)(2,1)}), (bf16[384,384]{1,0:T(8,128)(2,1)}, bf16[384,384]{1,0:T(8,128)(2,1)}, bf16[384,384]{1,0:T(8,128)(2,1)})) %all-reduce.9.cloned.1.call-update) | async-done | bytes 884752 | tf_op jit(solution)/shard_map/psum | solution.py:53
  203.2 1.9 fusion.2
  205.1 1.5 add_convert_fusion
  206.6 4.6 %all-to-all-start.5 = ((bf16[8,2,24,1024]{3,2,1,0:T(8,128)(2,1)}), bf16[8,2,24,1024]{3,2,1,0:T(8,128)(2,1)S(1)}, u32[]{:S(2)}, u32[]{:S(2)}) async-start(bf16[8,2,24,1024]{3,2,1,0:T(8,128)(2,1)} %bitcast.25), calls=%async_computation.5 | async-start | bytes 1572864 | tf_op jit(solution)/shard_map/all_to_all | solution.py:40
  211.4 20.7 %all-to-all-done.5 = bf16[8,2,24,1024]{3,2,1,0:T(8,128)(2,1)S(1)} async-done(((bf16[8,2,24,1024]{3,2,1,0:T(8,128)(2,1)}), bf16[8,2,24,1024]{3,2,1,0:T(8,128)(2,1)S(1)}, u32[]{:S(2)}, u32[]{:S(2)}) %all-to-all-start.5) | async-done | bytes 786464 | tf_op jit(solution)/shard_map/all_to_all | solution.py:40
  232.2 0.9 gather_fusion.6
  233.0 0.9 gather_fusion.7
  233.9 0.2 convert_add_fusion
  234.1 0.3 reshape.182
  234.4 0.6 reduce_sum.77
  235.0 0.1 multiply_reduce_fusion
  235.1 4.9 %psum.71 = f32[64]{0:T(128)S(1)} all-reduce(f32[64]{0:T(128)S(1)} %multiply_reduce_fusion), channel_id=1, replica_groups=mesh['section'=2,'tensor'=2,'expert'=8] {'tensor'}, use_global_device_ids=true, to_apply=%region_21.23 | all-reduce | flops 64 | bytes 512 | tf_op jit(solution)/shard_map/psum | solution.py:130
  240.2 0.7 maximum_bitcast_fusion
  (85 shorter events, 2.7 us)
Async XLA Ops:
  6.5 47.3 %copy-start = (bf16[1,1,1024,384]{3,2,1,0:T(8,128)(2,1)S(1)}, bf16[1,1,1024,384]{3,2,1,0:T(8,128)(2,1)}, u32[]{:S(2)}) copy-start(bf16[1,1,1024,384]{3,2,1,0:T(8,128)(2,1)} %param.17) | copy-start | bytes 2359300
  18.2 7.2 %copy-start.1 = (bf16[1,64,1024]{2,1,0:T(8,128)(2,1)S(1)}, bf16[1,64,1024]{2,1,0:T(8,128)(2,1)}, u32[]{:S(2)}) copy-start(bf16[1,64,1024]{2,1,0:T(8,128)(2,1)} %param.12) | copy-start | bytes 393220
  20.0 17.9 %all-to-all-start.1 = ((bf16[8,24,1024]{2,1,0:T(8,128)(2,1)}), bf16[8,24,1024]{2,1,0:T(8,128)(2,1)S(1)}, u32[]{:S(2)}, u32[]{:S(2)}) async-start(bf16[8,24,1024]{2,1,0:T(8,128)(2,1)} %bitcast.10), calls=%async_computation.1 | async-start | bytes 786432 | tf_op jit(solution)/shard_map/all_to_all | solution.py:110
  25.4 1.0 copy-start.4
  37.9 15.9 %all-to-all-start = ((bf16[8,24,1024]{2,1,0:T(8,128)(2,1)}), bf16[8,24,1024]{2,1,0:T(8,128)(2,1)S(1)}, u32[]{:S(2)}, u32[]{:S(2)}) async-start(bf16[8,24,1024]{2,1,0:T(8,128)(2,1)} %fusion.1), calls=%async_computation | async-start | bytes 786432 | tf_op jit(solution)/shard_map/all_to_all | solution.py:111
  41.3 13.8 %copy-start.7 = (bf16[1,1,1024,384]{3,2,1,0:T(8,128)(2,1)S(1)}, bf16[1,1,1024,384]{3,2,1,0:T(8,128)(2,1)}, u32[]{:S(2)}) copy-start(bf16[1,1,1024,384]{3,2,1,0:T(8,128)(2,1)} %param.18) | copy-start | bytes 2359300
  41.4 52.3 %all-reduce.11.cloned.1.call-start = ((), (), s32[]{:S(2)}) async-start(), calls=%async_computation.7 | async-start | bytes 1769472 | tf_op jit(solution)/shard_map/psum | solution.py:53
  41.4 12.4 %collective-permute-start.1 = (bf16[8,24,1024]{2,1,0:T(8,128)(2,1)S(1)}, bf16[8,24,1024]{2,1,0:T(8,128)(2,1)S(1)}, u32[]{:S(2)}, u32[]{:S(2)}) collective-permute-start(bf16[8,24,1024]{2,1,0:T(8,128)(2,1)S(1)} %all-to-all-done.1), channel_id=1, source_target_pairs={{0,1},{1,0},{2,3},{3,2},{4,5},{5,4},{6,7},{7,6},{8,9},{9,8},{10,11... | collective-permute-start | bytes 1179656 | tf_op jit(solution)/shard_map/ppermute | solution.py:19
  53.8 2.7 %collective-permute-start = (bf16[8,24,1024]{2,1,0:T(8,128)(2,1)S(1)}, bf16[8,24,1024]{2,1,0:T(8,128)(2,1)S(1)}, u32[]{:S(2)}, u32[]{:S(2)}) collective-permute-start(bf16[8,24,1024]{2,1,0:T(8,128)(2,1)S(1)} %all-to-all-done), channel_id=1, source_target_pairs={{0,1},{1,0},{2,3},{3,2},{4,5},{5,4},{6,7},{7,6},{8,9},{9,8},{10,11... | collective-permute-start | bytes 1179656 | tf_op jit(solution)/shard_map/ppermute | solution.py:19
  55.2 1.4 copy-start.5
  93.7 1.9 copy-start.10
  93.7 1.9 copy-start.11
  97.1 25.6 %all-to-all-start.2 = ((bf16[8,2,24,1024]{3,2,1,0:T(8,128)(2,1)}), bf16[8,2,24,1024]{3,2,1,0:T(8,128)(2,1)S(1)}, u32[]{:S(2)}, u32[]{:S(2)}) async-start(bf16[8,2,24,1024]{3,2,1,0:T(8,128)(2,1)} %bitcast.14), calls=%async_computation.2 | async-start | bytes 1572864 | tf_op jit(solution)/shard_map/all_to_all | solution.py:40
  124.3 1.1 copy-start.2
  130.7 12.9 %copy-start.3 = (bf16[64,1024]{1,0:T(8,128)(2,1)S(1)}, bf16[64,1024]{1,0:T(8,128)(2,1)}, u32[]{:S(2)}) copy-start(bf16[64,1024]{1,0:T(8,128)(2,1)} %param.13) | copy-start | bytes 393220
  132.5 15.9 %all-to-all-start.4 = ((bf16[8,24,1024]{2,1,0:T(8,128)(2,1)}), bf16[8,24,1024]{2,1,0:T(8,128)(2,1)S(1)}, u32[]{:S(2)}, u32[]{:S(2)}) async-start(bf16[8,24,1024]{2,1,0:T(8,128)(2,1)} %bitcast.23), calls=%async_computation.4 | async-start | bytes 786432 | tf_op jit(solution)/shard_map/all_to_all | solution.py:110
  135.9 7.7 %collective-permute-start.2 = (bf16[64,1024]{1,0:T(8,128)(2,1)S(1)}, bf16[64,1024]{1,0:T(8,128)(2,1)S(1)}, u32[]{:S(2)}, u32[]{:S(2)}) collective-permute-start(bf16[64,1024]{1,0:T(8,128)(2,1)S(1)} %get-tuple-element.23), channel_id=1, source_target_pairs={{16,0},{17,1},{18,2},{19,3},{20,4},{21,5},{22,6},{23,7},{24,8},{25... | collective-permute-start | bytes 393224 | tf_op jit(solution)/shard_map/ppermute | solution.py:25
  148.4 15.9 %all-to-all-start.3 = ((bf16[8,24,1024]{2,1,0:T(8,128)(2,1)}), bf16[8,24,1024]{2,1,0:T(8,128)(2,1)S(1)}, u32[]{:S(2)}, u32[]{:S(2)}) async-start(bf16[8,24,1024]{2,1,0:T(8,128)(2,1)} %fusion), calls=%async_computation.3 | async-start | bytes 786432 | tf_op jit(solution)/shard_map/all_to_all | solution.py:111
  151.8 51.3 %all-reduce.9.cloned.1.call-start = ((), (), s32[]{:S(2)}) async-start(), calls=%async_computation.6 | async-start | bytes 1769472 | tf_op jit(solution)/shard_map/psum | solution.py:53
  152.1 12.2 %collective-permute-start.4 = (bf16[8,24,1024]{2,1,0:T(8,128)(2,1)S(1)}, bf16[8,24,1024]{2,1,0:T(8,128)(2,1)S(1)}, u32[]{:S(2)}, u32[]{:S(2)}) collective-permute-start(bf16[8,24,1024]{2,1,0:T(8,128)(2,1)S(1)} %all-to-all-done.4), channel_id=1, source_target_pairs={{0,1},{1,0},{2,3},{3,2},{4,5},{5,4},{6,7},{7,6},{8,9},{9,8},{10,11... | collective-permute-start | bytes 1179656 | tf_op jit(solution)/shard_map/ppermute | solution.py:19
  164.3 1.4 copy-start.8
  164.3 2.7 %collective-permute-start.3 = (bf16[8,24,1024]{2,1,0:T(8,128)(2,1)S(1)}, bf16[8,24,1024]{2,1,0:T(8,128)(2,1)S(1)}, u32[]{:S(2)}, u32[]{:S(2)}) collective-permute-start(bf16[8,24,1024]{2,1,0:T(8,128)(2,1)S(1)} %all-to-all-done.3), channel_id=1, source_target_pairs={{0,1},{1,0},{2,3},{3,2},{4,5},{5,4},{6,7},{7,6},{8,9},{9,8},{10,11... | collective-permute-start | bytes 1179656 | tf_op jit(solution)/shard_map/ppermute | solution.py:19
  165.7 1.4 copy-start.6
  203.2 1.9 copy-start.9
  203.2 1.9 copy-start.12
  203.2 2.0 copy-start.13
  206.6 25.6 %all-to-all-start.5 = ((bf16[8,2,24,1024]{3,2,1,0:T(8,128)(2,1)}), bf16[8,2,24,1024]{3,2,1,0:T(8,128)(2,1)S(1)}, u32[]{:S(2)}, u32[]{:S(2)}) async-start(bf16[8,2,24,1024]{3,2,1,0:T(8,128)(2,1)} %bitcast.25), calls=%async_computation.5 | async-start | bytes 1572864 | tf_op jit(solution)/shard_map/all_to_all | solution.py:40
Sparse Core Ops, SparseCore 0:
  58.0 35.6 all-reduce.10
  168.5 34.6 all-reduce.8
where the time goes:
time: 249 us; the launch traced here: 248 us
  waiting for transfers between devices  151 us (61%)
  starting transfers between devices  27.1 us (11%)
  blocking collectives  15.7 us (6%)
  local copies, waits for them, and re-layouts  15.3 us (6%)
  matrix products  14.6 us (6%)
  between operations  13.9 us (6%)
  other arithmetic  9.61 us (4%)
    psum x2, waiting for transfers between devices, expert_rows(): lax.psum(hidden_part.astype(jnp.bfloat16), 'tensor').astype(jnp.float32)  69.7 us
    all_to_all x2, waiting for transfers between devices, send_back(): lax.all_to_all(grad_rows, 'expert', split_axis=0, concat_axis=0, tiled=True)  40.6 us
    all_to_all x2, waiting for transfers between devices, layer_step(): lax.all_to_all(send_grads, 'expert', split_axis=0, concat_axis=0, tiled=T...  24 us
    all_to_all x2, waiting for transfers between devices, layer_step(): lax.all_to_all(send_normed, 'expert', split_axis=0, concat_axis=0, tiled=...  12.1 us
    psum x2, blocking collectives, layer_step(): inner = lax.psum(jnp.sum(normed[micro] * scaled, axis=1), 'tensor')  9.85 us
    dot_general x6, matrix products, contract_last(): lax.dot_general(left, right, (((1,), (1,)), ((), ())), preferred_element_...  9.4 us
    all_to_all x2, starting transfers between devices, send_back(): lax.all_to_all(grad_rows, 'expert', split_axis=0, concat_axis=0, tiled=True)  9.22 us
    all_to_all x2, starting transfers between devices, layer_step(): lax.all_to_all(send_normed, 'expert', split_axis=0, concat_axis=0, tiled=...  8.84 us
  transfers between devices with their start and end apart: 13, of which 9 were waited for; matrix products, arithmetic and copies ran while one was open for 6% of the time, Pallas kernels for 0%

commit v1 on v0

v1 whole, which is shorter than its diff:
```python
import jax
import jax.numpy as jnp
from jax import lax
from jax.experimental import pallas as pl
from jax.experimental.pallas import tpu as pltpu
from jax.sharding import PartitionSpec as P

epsilon = 1e-06
MESH = pl.DeviceIdType.MESH
bf16 = jnp.bfloat16
f32 = jnp.float32


def contract_last(left, right):
    return lax.dot_general(left, right, (((1,), (1,)), ((), ())), preferred_element_type=f32)


def contract_first(left, right):
    return lax.dot_general(left, right, (((0,), (0,)), ((), ())), preferred_element_type=f32)


def dot(left, right):
    return jnp.dot(left, right, preferred_element_type=f32)


def make_kernel(sections, tensors, experts, capacity):

    def kernel(
        saved, cot_in, loss_grad, ids, weights, gain, wg_hbm, wu_hbm, wd_hbm, out,
        wg, wu, wd, w_sem, choose, picked, rows_out, rows, part_gu, part_h,
        y_send_gu, y_recv_gu, y_send_h, y_recv_h, grads, piece, pair_send, pair_recv,
        ret_send, ret_recv, sq_send, sq_recv, in_send, in_recv, sec_recv,
        d_s, d_r, f_s, f_r, y_s, y_r, a_s, a_r, p_s, p_r, r_s, r_r, q_s, q_r, i_s, i_r, c_s, c_r,
    ):
        s = lax.axis_index("section")
        t = lax.axis_index("tensor")
        x = lax.axis_index("expert")
        e, q = x // 2, x % 2
        ot, oq = 1 - t, 1 - q
        tok = saved.shape[2]
        feat = saved.shape[3]
        top = ids.shape[3]
        hid = wg.shape[1]
        model = feat * tensors

        loads = [
            pltpu.make_async_copy(wd_hbm.at[0, 0], wd, w_sem.at[0]),
            pltpu.make_async_copy(wg_hbm.at[0, 0], wg, w_sem.at[1]),
            pltpu.make_async_copy(wu_hbm.at[0, 0], wu, w_sem.at[2]),
        ]
        for load in loads:
            load.start()

        def expert_at(j):
            return lax.rem(e + j, experts)

        def source_at(j):
            return lax.rem(e + experts - j, experts)

        lane_peer = lambda chip: (s, t, 2 * chip + q)
        partner = (s, t, 2 * e + oq)
        y_peer = (s, ot, x)

        barrier = pltpu.get_barrier_semaphore()
        greet = [lane_peer(expert_at(j)) for j in range(1, experts)] + [partner, y_peer]
        for device in greet:
            pl.semaphore_signal(barrier, inc=1, device_id=device, device_id_type=MESH)

        @pl.when(s > 0)
        def _():
            pl.semaphore_signal(barrier, inc=1, device_id=(s - 1, t, x), device_id_type=MESH)

        @pl.when(s < sections - 1)
        def _():
            pl.semaphore_signal(barrier, inc=1, device_id=(s + 1, t, x), device_id_type=MESH)

        def remote(src, dst, send, recv, device):
            return pltpu.make_async_remote_copy(
                src_ref=src, dst_ref=dst, send_sem=send, recv_sem=recv,
                device_id=device, device_id_type=MESH,
            )

        def direct(m, k, j):
            return remote(
                rows_out.at[m, k, j], rows.at[m, k, j, q], d_s.at[m, k, j], d_r.at[m, k, j],
                lane_peer(expert_at(j)),
            )

        def forward(m, k, j):
            return remote(
                rows.at[m, k, j, q], rows.at[m, k, j, q], f_s.at[m, k, j], f_r.at[m, k, j], partner
            )

        def exchange(m, k, j):
            src, dst = ((y_send_gu, y_recv_gu), (y_send_h, y_recv_h))[k]
            return remote(src.at[m, j], dst.at[m, j], y_s.at[m, k, j], y_r.at[m, k, j], y_peer)

        def share(m, j):
            return remote(
                grads.at[m, j, t], grads.at[m, j, t], a_s.at[m, j], a_r.at[m, j], y_peer
            )

        def pair(m, j):
            return remote(
                pair_send.at[m, j], pair_recv.at[m, j], p_s.at[m, j], p_r.at[m, j], partner
            )

        def give_back(m, j):
            return remote(
                ret_send.at[m, j], ret_recv.at[m, j], r_s.at[m, j], r_r.at[m, j],
                lane_peer(source_at(j)),
            )

        def squares_copy():
            return remote(sq_send, sq_recv, q_s, q_r, y_peer)

        def inner_copy(m):
            return remote(in_send.at[m], in_recv.at[m], i_s.at[m], i_r.at[m], y_peer)

        def section_copy():
            return remote(out.at[0, 0], sec_recv, c_s, c_r, (s - 1, t, x))

        started = []

        def start(copy):
            copy.start()
            started.append(copy)

        lane = lax.broadcasted_iota(jnp.int32, (tok, 128), 1)
        named = e + lane
        named = jnp.where(named >= experts, named - experts, named)
        named = jnp.where(lane < experts, named, -1)
        earlier = (
            lax.broadcasted_iota(jnp.int32, (tok, tok), 1)
            < lax.broadcasted_iota(jnp.int32, (tok, tok), 0)
        ).astype(f32).astype(bf16)
        slot = lax.broadcasted_iota(jnp.int32, (tok, capacity), 1).astype(f32)
        weight_of = []
        for m in range(2):
            hit = jnp.zeros((tok, 128), f32)
            weight = jnp.zeros((tok, 128), f32)
            for k in range(top):
                same = (ids[0, m, :, k : k + 1] == named).astype(f32)
                hit = hit + same
                weight = weight + same * weights[0, m, :, k : k + 1]
            position = dot(earlier, hit.astype(bf16))
            for j in range(experts):
                chosen = (position[:, j : j + 1] == slot).astype(f32) * hit[:, j : j + 1]
                choose[m, j] = chosen.astype(bf16)
            picked[m] = weight
        square = []
        for m in range(2):
            values = saved[0, m].astype(f32)
            square.append(jnp.sum(values * values, axis=1, keepdims=True))
        sq_send[...] = jnp.where(lane < 64, square[0], square[1])

        neighbours = (s > 0).astype(jnp.int32) + (s < sections - 1).astype(jnp.int32)
        pl.semaphore_wait(barrier, len(greet) + neighbours)

        start(squares_copy())

        def dispatch(m, k, value_of):
            for j in list(range(1, experts)) + [0]:
                packed = contract_first(choose[m, j], value_of(j)).astype(bf16)
                if j == 0:
                    rows[m, k, j, q] = packed
                    start(forward(m, k, j))
                else:
                    rows_out[m, k, j] = packed
                    start(direct(m, k, j))

        def dispatch_grads(m, incoming):
            dispatch(m, 1, lambda j: (picked[m][:, j : j + 1] * incoming).astype(bf16))

        dispatch_grads(0, cot_in[0].astype(f32))
        squares_copy().wait_recv()
        total = sq_send[...] + sq_recv[...]
        roots = [
            jnp.sqrt(total[:, 64 * m : 64 * m + 1] / model + epsilon) for m in range(2)
        ]

        def normed_of(m):
            return saved[0, m].astype(f32) / roots[m]

        for m in range(2):
            value = (normed_of(m) * gain[...]).astype(bf16)
            dispatch(m, 0, lambda j: value)

        for load in loads:
            load.wait()

        def receive(m, k, j):
            if j > 0:
                direct(m, k, j).wait_recv()
                start(forward(m, k, j))

        def consume(m, k, j):
            forward(m, k, j).wait_recv()
            flat = rows[m, k, j].reshape(2 * capacity, feat)
            if k == 0:
                part_gu[m, j, :, :, :hid] = dot(flat, wg[...]).reshape(2, capacity, hid)
                part_gu[m, j, :, :, hid:] = dot(flat, wu[...]).reshape(2, capacity, hid)
                y_send_gu[m, j] = part_gu[m, j, ot].astype(bf16)
            else:
                part_h[m, j] = contract_last(flat, wd[...]).reshape(2, capacity, hid)
                y_send_h[m, j] = part_h[m, j, ot].astype(bf16)
            start(exchange(m, k, j))

        def stream(items):
            last = None
            for item in items:
                receive(*item)
                if last is not None:
                    consume(*last)
                last = item
            consume(*last)

        def activate(m, j):
            exchange(m, 0, j).wait_recv()
            exchange(m, 1, j).wait_recv()
            both = part_gu[m, j, t] + y_recv_gu[m, j].astype(f32)
            hidden = part_h[m, j, t] + y_recv_h[m, j].astype(f32)
            gate, up = both[:, :hid], both[:, hid:]
            sigma = jax.nn.sigmoid(gate)
            grads[m, j, t, :, :hid] = (
                hidden * up * (sigma * (1.0 + gate * (1.0 - sigma)))
            ).astype(bf16)
            grads[m, j, t, :, hid:] = (hidden * (gate * sigma)).astype(bf16)
            start(share(m, j))

        def pieces(m, j):
            share(m, j).wait_recv()
            flat = grads[m, j].reshape(2 * capacity, 2 * hid)
            done = contract_last(flat[:, :hid], wg[...]) + contract_last(flat[:, hid:], wu[...])
            piece[m, j] = done.reshape(2, capacity, feat)
            pair_send[m, j] = piece[m, j, oq].astype(bf16)
            start(pair(m, j))

        def finish(m, j):
            pair(m, j).wait_recv()
            summed = (piece[m, j, q] + pair_recv[m, j].astype(f32)).astype(bf16)
            if j == 0:
                ret_recv[m, j] = summed
            else:
                ret_send[m, j] = summed
                start(give_back(m, j))

        def send_back(m):
            order = list(range(1, experts)) + [0]
            last = None
            for j in order:
                pieces(m, j)
                if last is not None:
                    finish(m, last)
                last = j
            finish(m, last)

        def combine(m, incoming):
            cot = dot(choose[m, 0], ret_recv[m, 0])
            for j in range(1, experts):
                give_back(m, j).wait_recv()
                cot = cot + dot(choose[m, j], ret_recv[m, j])
            scaled = gain[...] * cot
            normed = normed_of(m)
            own = jnp.sum(normed * scaled, axis=1, keepdims=True)
            in_send[m] = jnp.broadcast_to(own, (tok, 128))
            start(inner_copy(m))
            inner_copy(m).wait_recv()
            inner = (in_send[m] + in_recv[m])[:, :1]
            out[0, m] = (
                incoming + (scaled - normed * (inner / model)) / roots[m]
            ).astype(bf16)

        js = list(range(experts))
        stream([(0, 1, j) for j in js] + [(0, 0, j) for j in js])
        for j in js[1:] + [0]:
            activate(0, j)
        stream([(1, 0, j) for j in js])
        send_back(0)
        combine(0, cot_in[0].astype(f32))

        @pl.when(s > 0)
        def _():
            section_copy().start()

        @pl.when(s < sections - 1)
        def _():
            section_copy().wait_recv()

        @pl.when(s == sections - 1)
        def _():
            sec_recv[...] = loss_grad[...]

        incoming = sec_recv[...].astype(f32)
        dispatch_grads(1, incoming)
        stream([(1, 1, j) for j in js])
        for j in js[1:] + [0]:
            activate(1, j)
        send_back(1)
        combine(1, incoming)

        for copy in started:
            copy.wait_send()

        @pl.when(s > 0)
        def _():
            section_copy().wait_send()

    return kernel


def solution(mesh):
    sections, tensors = mesh.shape["section"], mesh.shape["tensor"]
    experts = mesh.shape["expert"] // 2

    def local(saved, cot_in, loss_grad, ids, weights, gain, wg, wu, wd):
        tok, feat = saved.shape[2], saved.shape[3]
        hid = wg.shape[3]
        named = 3 * tok * ids.shape[3] // (2 * experts)
        cap = -(-named // 16) * 16
        vmem = pl.BlockSpec(memory_space=pltpu.VMEM)
        hbm = pl.BlockSpec(memory_space=pl.ANY)
        dma = pltpu.SemaphoreType.DMA
        scratch = [
            pltpu.VMEM((feat, hid), bf16), pltpu.VMEM((feat, hid), bf16),
            pltpu.VMEM((hid, feat), bf16), dma((3,)),
            pltpu.VMEM((2, experts, tok, cap), bf16), pltpu.VMEM((2, tok, 128), f32),
            pltpu.VMEM((2, 2, experts, cap, feat), bf16),
            pltpu.VMEM((2, 2, experts, 2, cap, feat), bf16),
            pltpu.VMEM((2, experts, 2, cap, 2 * hid), f32),
            pltpu.VMEM((2, experts, 2, cap, hid), f32),
            pltpu.VMEM((2, experts, cap, 2 * hid), bf16),
            pltpu.VMEM((2, experts, cap, 2 * hid), bf16),
            pltpu.VMEM((2, experts, cap, hid), bf16),
            pltpu.VMEM((2, experts, cap, hid), bf16),
            pltpu.VMEM((2, experts, 2, cap, 2 * hid), bf16),
            pltpu.VMEM((2, experts, 2, cap, feat), f32),
            pltpu.VMEM((2, experts, cap, feat), bf16),
            pltpu.VMEM((2, experts, cap, feat), bf16),
            pltpu.VMEM((2, experts, cap, feat), bf16),
            pltpu.VMEM((2, experts, cap, feat), bf16),
            pltpu.VMEM((tok, 128), f32), pltpu.VMEM((tok, 128), f32),
            pltpu.VMEM((2, tok, 128), f32), pltpu.VMEM((2, tok, 128), f32),
            pltpu.VMEM((tok, feat), bf16),
        ]
        for shape in [(2, 2, experts)] * 6 + [(2, experts)] * 6:
            scratch.append(dma(shape))
        scratch += [dma, dma, dma((2,)), dma((2,)), dma, dma]
        return pl.pallas_call(
            make_kernel(sections, tensors, experts, cap),
            out_shape=jax.ShapeDtypeStruct((1, 2, tok, feat), bf16),
            in_specs=[vmem] * 6 + [hbm] * 3,
            out_specs=vmem,
            scratch_shapes=scratch,
            compiler_params=pltpu.CompilerParams(
                collective_id=0, has_side_effects=True, vmem_limit_bytes=62 * 1024 * 1024
            ),
            name="expert_back",
        )(saved, cot_in, loss_grad, ids, weights, gain, wg, wu, wd)

    in_specs = (
        P("section", None, "expert", "tensor"),
        P("section", "expert", "tensor"),
        P("expert", "tensor"),
        P("section", None, "expert", None),
        P("section", None, "expert", None),
        P("section", "tensor"),
        P("section", "expert", "tensor", None),
        P("section", "expert", "tensor", None),
        P("section", "expert", None, "tensor"),
    )
    out_specs = P("section", None, "expert", "tensor")
    return jax.shard_map(local, mesh=mesh, in_specs=in_specs, out_specs=out_specs, check_vma=False)
```

time: 249 us -> 95.6 us (0.38)
  waiting for transfers between devices: 151 us -> 0 us
  Pallas kernels: 0 us -> 91.6 us
  starting transfers between devices: 27.1 us -> 0 us
  blocking collectives: 15.7 us -> 0 us
  matrix products: 14.6 us -> 0 us
  between operations: 13.9 us -> 0.01 us
  local copies, waits for them, and re-layouts: 15.3 us -> 3.84 us
  other arithmetic: 9.61 us -> 0 us
    pallas_call x0 -> x1, Pallas kernels: none -> 91.6 us  [local(): pl.pallas_call(make_kernel(sections, tensors, experts, cap), out_shape=ja...]
    all_to_all x6 -> x0, waiting for transfers between devices: 76.7 us -> none  [the longest x2 40.6 us: send_back(): lax.all_to_all(grad_rows, 'expert', split_axis=0, concat_axis=0, tiled=True)]
    psum x2 -> x0, waiting for transfers between devices: 69.7 us -> none  [expert_rows(): lax.psum(hidden_part.astype(jnp.bfloat16), 'tensor').astype(jnp.float32)]
    all_to_all x6 -> x0, starting transfers between devices: 25 us -> none  [the longest x2 9.22 us: send_back(): lax.all_to_all(grad_rows, 'expert', split_axis=0, concat_axis=0, tiled=True)]
    psum x3 -> x0, blocking collectives: 15.7 us -> none  [the longest x2 9.85 us: layer_step(): inner = lax.psum(jnp.sum(normed[micro] * scaled, axis=1), 'tensor')]
    dot_general x10 -> x0, matrix products: 14.6 us -> none  [the longest x6 9.4 us: contract_last(): lax.dot_general(left, right, (((1,), (1,)), ((), ())), preferred_element_...]
    gather x8 -> x0, local copies, waits for them, and re-layouts: 9 us -> none  [the longest x2 3.53 us: layer_step(): send_normed = padded_input[token_of]]
    ppermute x5 -> x0, waiting for transfers between devices: 5.09 us -> none  [the longest x1 5.08 us: passed_along(): return lax.ppermute(array, axis, pairs)]
  transfers between devices with their start and end apart: 13 -> 0, of which waited for: 9 -> 0; matrix products, arithmetic and copies ran while one was open for 6% -> 0% of each run, Pallas kernels for 0% -> 0%
where the time goes in v1:
time: 95.6 us; the launch traced here: 95.4 us
  Pallas kernels  91.6 us (96%)
  local copies, waits for them, and re-layouts  3.84 us (4%)
    pallas_call x1, Pallas kernels, local(): pl.pallas_call(make_kernel(sections, tensors, experts, cap), out_shape=ja...  91.6 us
    unnamed x5, local copies, waits for them, and re-layouts  3.84 us

profile of v1, /device:TPU:0, one launch (start us, length us, event | category | flops | bytes accessed | tf_op | source)
XLA Modules:
  0.0 95.4 jit_solution(281153937363573547)
XLA Ops:
  0.0 0.0 copy-start
  0.0 1.4 %copy.10.ids = s32[1,2,64,2]{3,2,1,0:T(8,128)} copy(s32[1,2,64,2]{2,3,1,0:T(2,128)} %param.12) | data formatting | bytes 2048 | tf_op args[3]
  1.4 0.0 copy-done
  1.4 0.7 copy.11.weights
  2.2 91.6 %expert_back.1 = bf16[1,2,64,1024]{3,2,1,0:T(8,128)(2,1)} custom-call(bf16[1,2,64,1024]{3,2,1,0:T(8,128)(2,1)} %saved.1, bf16[1,64,1024]{2,1,0:T(8,128)(2,1)} %cot_in.1, bf16[64,1024]{1,0:T(8,128)(2,1)} %loss_grad.1, s32[1,2,64,2]{3,2,1,0:T(8,128)} %copy.10.ids, f32[1,2,64,2]{3,2,1,0:T(8,128)} %copy.11.weights, f32[1,1024]{1,0:T(1,128)} %gain.1, ...), custom_call_target="tpu_custom_call" | custom-call | tf_op jit(solution)/shard_map/expert_back/pallas_call | solution.py:349
  93.8 1.7 %copy.13 = bf16[1,2,64,1024]{3,2,1,0:T(8,128)(2,1)} copy(bf16[1,2,64,1024]{3,2,1,0:T(8,128)(2,1)} %expert_back.1) | data formatting | bytes 524288
Async XLA Ops:
  0.0 1.4 %copy-start = (f32[1,2,64,2]{2,3,1,0:T(2,128)S(1)}, f32[1,2,64,2]{2,3,1,0:T(2,128)}, u32[]{:S(2)}) copy-start(f32[1,2,64,2]{2,3,1,0:T(2,128)} %param.13) | copy-start | bytes 3076

commit v2 on v1

--- a/solution.py
+++ b/solution.py
@@ -39,7 +39,7 @@
         ot, oq = 1 - t, 1 - q
         tok = saved.shape[2]
         feat = saved.shape[3]
-        top = ids.shape[3]
+        top = ids.shape[2]
         hid = wg.shape[1]
         model = feat * tensors
 
@@ -126,28 +126,29 @@
             copy.start()
             started.append(copy)
 
+        height = max(8, experts)
         lane = lax.broadcasted_iota(jnp.int32, (tok, 128), 1)
-        named = e + lane
+        named = e + lax.broadcasted_iota(jnp.int32, (height, tok), 0)
         named = jnp.where(named >= experts, named - experts, named)
-        named = jnp.where(lane < experts, named, -1)
-        earlier = (
-            lax.broadcasted_iota(jnp.int32, (tok, tok), 1)
-            < lax.broadcasted_iota(jnp.int32, (tok, tok), 0)
+        later = (
+            lax.broadcasted_iota(jnp.int32, (tok, tok), 0)
+            < lax.broadcasted_iota(jnp.int32, (tok, tok), 1)
         ).astype(f32).astype(bf16)
-        slot = lax.broadcasted_iota(jnp.int32, (tok, capacity), 1).astype(f32)
-        weight_of = []
+        slot = lax.broadcasted_iota(jnp.int32, (capacity, tok), 0).astype(f32)
         for m in range(2):
-            hit = jnp.zeros((tok, 128), f32)
-            weight = jnp.zeros((tok, 128), f32)
+            hit = jnp.zeros((height, tok), f32)
+            weight = jnp.zeros((height, tok), f32)
             for k in range(top):
-                same = (ids[0, m, :, k : k + 1] == named).astype(f32)
+                same = (ids[0, m, k : k + 1, :] == named).astype(f32)
                 hit = hit + same
-                weight = weight + same * weights[0, m, :, k : k + 1]
-            position = dot(earlier, hit.astype(bf16))
+                weight = weight + same * weights[0, m, k : k + 1, :]
+            position = dot(hit.astype(bf16), later)
             for j in range(experts):
-                chosen = (position[:, j : j + 1] == slot).astype(f32) * hit[:, j : j + 1]
+                chosen = (position[j : j + 1] == slot).astype(f32) * hit[j : j + 1]
                 choose[m, j] = chosen.astype(bf16)
-            picked[m] = weight
+                picked[m, j] = jnp.broadcast_to(
+                    jnp.sum(chosen * weight[j : j + 1], axis=1, keepdims=True), (capacity, 128)
+                )
         square = []
         for m in range(2):
             values = saved[0, m].astype(f32)
@@ -159,20 +160,22 @@
 
         start(squares_copy())
 
-        def dispatch(m, k, value_of):
-            for j in list(range(1, experts)) + [0]:
-                packed = contract_first(choose[m, j], value_of(j)).astype(bf16)
-                if j == 0:
-                    rows[m, k, j, q] = packed
-                    start(forward(m, k, j))
-                else:
-                    rows_out[m, k, j] = packed
-                    start(direct(m, k, j))
-
-        def dispatch_grads(m, incoming):
-            dispatch(m, 1, lambda j: (picked[m][:, j : j + 1] * incoming).astype(bf16))
-
-        dispatch_grads(0, cot_in[0].astype(f32))
+        def dispatch(m, k, j, value):
+            packed = dot(choose[m, j], value)
+            if k == 1:
+                packed = picked[m, j][:, :1] * packed
+            if j == 0:
+                rows[m, k, j, q] = packed.astype(bf16)
+                start(forward(m, k, j))
+            else:
+                rows_out[m, k, j] = packed.astype(bf16)
+                start(direct(m, k, j))
+
+        js = list(range(experts))
+        near = js[1 : experts // 2 + 1] + [0]
+        far = js[experts // 2 + 1 :]
+        for j in near:
+            dispatch(0, 1, j, cot_in[0])
         squares_copy().wait_recv()
         total = sq_send[...] + sq_recv[...]
         roots = [
@@ -182,9 +185,15 @@
         def normed_of(m):
             return saved[0, m].astype(f32) / roots[m]
 
-        for m in range(2):
-            value = (normed_of(m) * gain[...]).astype(bf16)
-            dispatch(m, 0, lambda j: value)
+        def expert_input(m):
+            return (normed_of(m) * gain[...]).astype(bf16)
+
+        value = expert_input(0)
+        for j in near:
+            dispatch(0, 0, j, value)
+        for j in far:
+            dispatch(0, 1, j, cot_in[0])
+            dispatch(0, 0, j, value)
 
         for load in loads:
             load.wait()
@@ -245,10 +254,14 @@
                 ret_send[m, j] = summed
                 start(give_back(m, j))
 
-        def send_back(m):
-            order = list(range(1, experts)) + [0]
+        def pipeline(m, kinds, between=()):
+            stream([(m, k, j) for k in kinds for j in js])
+            for j in js[1:] + [0]:
+                activate(m, j)
+            if between:
+                stream(between)
             last = None
-            for j in order:
+            for j in js[1:] + [0]:
                 pieces(m, j)
                 if last is not None:
                     finish(m, last)
@@ -256,10 +269,10 @@
             finish(m, last)
 
         def combine(m, incoming):
-            cot = dot(choose[m, 0], ret_recv[m, 0])
+            cot = contract_first(choose[m, 0], ret_recv[m, 0])
             for j in range(1, experts):
                 give_back(m, j).wait_recv()
-                cot = cot + dot(choose[m, j], ret_recv[m, j])
+                cot = cot + contract_first(choose[m, j], ret_recv[m, j])
             scaled = gain[...] * cot
             normed = normed_of(m)
             own = jnp.sum(normed * scaled, axis=1, keepdims=True)
@@ -271,18 +284,18 @@
                 incoming + (scaled - normed * (inner / model)) / roots[m]
             ).astype(bf16)
 
-        js = list(range(experts))
-        stream([(0, 1, j) for j in js] + [(0, 0, j) for j in js])
+        pipeline(0, (1, 0))
+        value = expert_input(1)
         for j in js[1:] + [0]:
-            activate(0, j)
-        stream([(1, 0, j) for j in js])
-        send_back(0)
+            dispatch(1, 0, j, value)
         combine(0, cot_in[0].astype(f32))
 
         @pl.when(s > 0)
         def _():
             section_copy().start()
 
+        stream([(1, 0, j) for j in js[: experts // 2]])
+
         @pl.when(s < sections - 1)
         def _():
             section_copy().wait_recv()
@@ -291,13 +304,11 @@
         def _():
             sec_recv[...] = loss_grad[...]
 
-        incoming = sec_recv[...].astype(f32)
-        dispatch_grads(1, incoming)
-        stream([(1, 1, j) for j in js])
         for j in js[1:] + [0]:
-            activate(1, j)
-        send_back(1)
-        combine(1, incoming)
+            dispatch(1, 1, j, sec_recv[...])
+        stream([(1, 0, j) for j in js[experts // 2 :]])
+        pipeline(1, (1,))
+        combine(1, sec_recv[...].astype(f32))
 
         for copy in started:
             copy.wait_send()
@@ -324,7 +335,7 @@
         scratch = [
             pltpu.VMEM((feat, hid), bf16), pltpu.VMEM((feat, hid), bf16),
             pltpu.VMEM((hid, feat), bf16), dma((3,)),
-            pltpu.VMEM((2, experts, tok, cap), bf16), pltpu.VMEM((2, tok, 128), f32),
+            pltpu.VMEM((2, experts, cap, tok), bf16), pltpu.VMEM((2, experts, cap, 128), f32),
             pltpu.VMEM((2, 2, experts, cap, feat), bf16),
             pltpu.VMEM((2, 2, experts, 2, cap, feat), bf16),
             pltpu.VMEM((2, experts, 2, cap, 2 * hid), f32),
@@ -356,7 +367,10 @@
                 collective_id=0, has_side_effects=True, vmem_limit_bytes=62 * 1024 * 1024
             ),
             name="expert_back",
-        )(saved, cot_in, loss_grad, ids, weights, gain, wg, wu, wd)
+        )(
+            saved, cot_in, loss_grad, ids.transpose(0, 1, 3, 2), weights.transpose(0, 1, 3, 2),
+            gain, wg, wu, wd,
+        )
 
     in_specs = (
         P("section", None, "expert", "tensor"),

time: 95.6 us -> 91 us (0.952)
  Pallas kernels: 91.6 us -> 89.2 us
  local copies, waits for them, and re-layouts: 3.84 us -> 1.67 us
    pallas_call x1, Pallas kernels: 91.6 us -> 89.2 us  [local(): pl.pallas_call(make_kernel(sections, tensors, experts, cap), out_shape=ja...]
    unnamed x5 -> x1, local copies, waits for them, and re-layouts: 3.84 us -> 1.67 us
where the time goes in v2:
time: 91 us; the launch traced here: 90.9 us
  Pallas kernels  89.2 us (98%)
  local copies, waits for them, and re-layouts  1.67 us (2%)
    pallas_call x1, Pallas kernels, local(): pl.pallas_call(make_kernel(sections, tensors, experts, cap), out_shape=ja...  89.2 us

profile of v2, /device:TPU:0, one launch (start us, length us, event | category | flops | bytes accessed | tf_op | source)
XLA Modules:
  0.0 90.9 jit_solution(4948665008938409633)
XLA Ops:
  0.0 89.2 %expert_back.1 = bf16[1,2,64,1024]{3,2,1,0:T(8,128)(2,1)} custom-call(bf16[1,2,64,1024]{3,2,1,0:T(8,128)(2,1)} %saved.1, bf16[1,64,1024]{2,1,0:T(8,128)(2,1)} %cot_in.1, bf16[64,1024]{1,0:T(8,128)(2,1)} %loss_grad.1, s32[1,2,2,64]{3,2,1,0:T(2,128)} %bitcast.2, f32[1,2,2,64]{3,2,1,0:T(2,128)} %bitcast.3, f32[1,1024]{1,0:T(1,128)} %gain.1, ...), custom_call_target="tpu_custom_call" | custom-call | tf_op jit(solution)/shard_map/expert_back/pallas_call | solution.py:360
  89.2 1.7 %copy.11 = bf16[1,2,64,1024]{3,2,1,0:T(8,128)(2,1)} copy(bf16[1,2,64,1024]{3,2,1,0:T(8,128)(2,1)} %expert_back.1) | data formatting | bytes 524288
